TPU v7x, 256 devices: a whole 4x4x8 slice. The times are simulated.
256 devices in a mesh: snap: 4 (over z_hi), param: 64 (over z_lo, x, y, core).
Axes of the slice: x: 4, y: 4, z: 8 (z_hi: 4, z_lo: 2; z = z_hi * 2 + z_lo), core: 2. Of those that a mesh axis runs over, the one named last changes fastest.
Arguments:
- snapshots: bfloat16 [256, 4096, 1024], P('snap', 'param'), as said below
- coeffs: float32 [16, 256], P(None, 'snap'), may hold values from -0.375 to 0.375
Outputs:
- averages: float32 [16, 4096, 1024], P(None, 'param', 'snap')
- width_norms: float32 [16], replicated
Inputs may be any that keep to these rules, and one draw needn't show every extreme that they name: `snapshots`: stored snapshot weights, finite.
All inputs are finite; a program needn't handle non-finite values.
Results may differ from a plain program's by a relative error of at most 0.0003.
Values may be sent and summed in bfloat16 or wider, within the bound.
A program may use at most 64 MiB of HBM per device.

v0:
```python
import functools

import jax
import jax.numpy as jnp
from jax import lax
from jax.sharding import Mesh
from jax.sharding import PartitionSpec as P

SNAP_PARAM = ("snap", "param_0", "param_1", "param_2", "param_3")
PARAM = ("param_0", "param_1", "param_2", "param_3")


def one_axis_at_a_time(shard, axes):
    return functools.reduce(lax.psum, axes, shard)


def combine(weights, stored):
    flat = stored.reshape(stored.shape[0], stored.shape[1] * stored.shape[2]).astype(jnp.float32)
    product = jnp.dot(
        weights, flat, precision=lax.Precision.HIGHEST, preferred_element_type=jnp.float32
    )
    return product.reshape(weights.shape[0], stored.shape[1], stored.shape[2])


def on_device(snapshots, coeffs):
    partial_value = combine(coeffs, snapshots)
    averages = lax.psum_scatter(partial_value, "snap", scatter_dimension=2, tiled=True)
    squares = jnp.sum(averages * averages, axis=(1, 2))
    total = one_axis_at_a_time(squares, SNAP_PARAM)
    entries = averages.shape[1] * averages.shape[2] * lax.axis_size("snap") * lax.axis_size(PARAM)
    width_norms = jnp.sqrt(total / jnp.float32(entries))
    return (averages, width_norms)


def solution(mesh):
    split = Mesh(
        mesh.devices.reshape(mesh.shape["snap"], 2, 4, 4, 2),
        ("snap", "param_0", "param_1", "param_2", "param_3"),
    )
    placed = (P("snap", PARAM, None), P(None, "snap"))
    return jax.shard_map(
        on_device,
        mesh=split,
        in_specs=placed,
        out_specs=(P(None, PARAM, "snap"), P()),
        check_vma=False,
    )
```

profile of v0, /device:TPU:1, one launch (start us, length us, event | category | flops | bytes accessed | tf_op | source)
XLA Modules:
  0.0 164.7 jit_solution(15653537481849412635)
XLA Ops:
  7.2 0.0 copy-start
  7.2 0.0 reduce-scatter.2.cloned.1.call-start
  7.2 0.6 copy-done
  7.9 17.1 %fusion = f32[16,64,1024]{2,0,1:T(8,128)} fusion(f32[16,64]{1,0:T(8,128)S(1)} %copy-done, bf16[8,8,64,1024]{3,2,1,0:T(8,128)(2,1)} %bitcast.14), kind=kOutput, calls=%fused_computation | convolution fusion | flops 805306368 | bytes 12587008 | tf_op jit(solution)/shard_map/dot_general | solution.py:19
  25.0 0.0 reduce-scatter.2.cloned.1.call-update
  25.0 88.4 %reduce-scatter.2.cloned.1.call-done = f32[16,64,256]{2,0,1:T(8,128)} async-done(((f32[16,64,1024]{2,0,1:T(8,128)}), f32[16,64,256]{2,0,1:T(8,128)}) %reduce-scatter.2.cloned.1.call-update) | async-done | bytes 1048592 | tf_op jit(solution)/shard_map/reduce_scatter | solution.py:27
  113.4 1.5 multiply_reduce_fusion
  114.9 9.1 %psum.35 = f32[16]{0:T(128)S(1)} all-reduce(f32[16]{0:T(128)S(1)} %multiply_reduce_fusion), channel_id=1, replica_groups=mesh['snap'=4,'param_0'=2,'param_1'=4,'param_2'=4,'param_3'=2] {'snap'}, use_global_device_ids=true, to_apply=%region_2.0 | all-reduce | flops 16 | bytes 128 | tf_op jit(solution)/shard_map/psum | solution.py:14
  123.9 3.8 %psum.36 = f32[16]{0:T(128)S(1)} all-reduce(f32[16]{0:T(128)S(1)} %psum.35), channel_id=1, replica_groups=mesh['snap'=4,'param_0'=2,'param_1'=4,'param_2'=4,'param_3'=2] {'param_0'}, use_global_device_ids=true, to_apply=%region_3.0 | all-reduce | flops 16 | bytes 128 | tf_op jit(solution)/shard_map/psum | solution.py:14
  127.7 8.4 %psum.37 = f32[16]{0:T(128)S(1)} all-reduce(f32[16]{0:T(128)S(1)} %psum.36), channel_id=1, replica_groups=mesh['snap'=4,'param_0'=2,'param_1'=4,'param_2'=4,'param_3'=2] {'param_1'}, use_global_device_ids=true, to_apply=%region_4.0 | all-reduce | flops 16 | bytes 128 | tf_op jit(solution)/shard_map/psum | solution.py:14
  136.1 8.4 %psum.38 = f32[16]{0:T(128)S(1)} all-reduce(f32[16]{0:T(128)S(1)} %psum.37), channel_id=1, replica_groups=mesh['snap'=4,'param_0'=2,'param_1'=4,'param_2'=4,'param_3'=2] {'param_2'}, use_global_device_ids=true, to_apply=%region_5.0 | all-reduce | flops 16 | bytes 128 | tf_op jit(solution)/shard_map/psum | solution.py:14
  144.5 10.0 %psum.39 = f32[16]{0:T(128)S(1)} all-reduce(f32[16]{0:T(128)S(1)} %psum.38), channel_id=1, replica_groups=mesh['snap'=4,'param_0'=2,'param_1'=4,'param_2'=4,'param_3'=2] {'param_3'}, use_global_device_ids=true, to_apply=%region_6.0 | all-reduce | flops 16 | bytes 128 | tf_op jit(solution)/shard_map/psum | solution.py:14
  154.5 0.5 multiply_sqrt_fusion
  155.0 2.8 %copy.6 = f32[16,64,256]{2,1,0:T(8,128)} copy(f32[16,64,256]{2,0,1:T(8,128)} %reduce-scatter.2.cloned.1.call-done) | data formatting | bytes 2097152
Async XLA Ops:
  7.2 0.7 copy-start
  7.2 106.2 %reduce-scatter.2.cloned.1.call-start = ((), (), s32[]{:S(2)}) async-start(), calls=%async_computation.1 | async-start | bytes 5242880 | tf_op jit(solution)/shard_map/reduce_scatter | solution.py:27
Sparse Core Ops, SparseCore 0:
  25.2 88.2 reduce-scatter.1
where the time goes:
time: 165 us
  waiting for transfers between devices  88.4 us (54%)
  blocking collectives  39.6 us (24%)
  matrix products  17.1 us (10%)
  between operations  14 us (8%)
  local copies, waits for them, and re-layouts  3.45 us (2%)
  other arithmetic  1.99 us (1%)
    reduce_scatter x1, waiting for transfers between devices, on_device(): lax.psum_scatter(partial_value, 'snap', scatter_dimension=2, tiled=True)  88.4 us
    psum x5, blocking collectives, one_axis_at_a_time(): return functools.reduce(lax.psum, axes, shard)  39.6 us
    dot_general x1, matrix products, combine(): jnp.dot(weights, flat, precision=lax.Precision.HIGHEST, preferred_element...  17.1 us
    unnamed x3, local copies, waits for them, and re-layouts  3.45 us
  transfers between devices with their start and end apart: 1, of which 1 were waited for; matrix products, arithmetic and copies ran while one was open for 0% of the time, Pallas kernels for 0%

commit v1 on v0

v1 whole, which is shorter than its diff:
```python
import functools

import jax
import jax.numpy as jnp
from jax import lax
from jax.experimental import pallas as pl
from jax.experimental.pallas import tpu as pltpu
from jax.sharding import Mesh
from jax.sharding import PartitionSpec as P

MESH = pl.DeviceIdType.MESH
PARAM = ("zlo", "x", "y", "core")
ROWS = 16
LEAST = -125.0
SPAN = 251.5
TINY = 1e-37


def encode(value):
    size = jnp.abs(value)
    largest = jnp.max(jnp.max(size, axis=0), axis=0, keepdims=True)
    largest = jnp.maximum(largest, TINY)
    inverse = 1.0 / largest
    power = jnp.exp2((size * inverse[None]) * SPAN + LEAST)
    return jnp.where(value < 0, -power, power).astype(jnp.bfloat16), largest


def decode(codes, largest):
    code = codes.astype(jnp.float32)
    size = (jnp.log2(jnp.abs(code)) - LEAST) * (largest * (1.0 / SPAN))[None]
    return jnp.where(code < 0, -size, size)


def tile_of(i):
    return (i % 2) * 2 + i // 2, 2 * (i % 2) - 1


def kernel(sizes, coeffs_hbm, snap_hbm, avg_hbm, norm_ref,
           coef, stage, kron, share, sent, sent_max, got, got_max, total, squares,
           note, seen1, seen2,
           coef_sem, stage_sem, out_sem, send_sem, send_max_sem, recv_sem, recv_max_sem,
           note1_send, note1_recv, note2_send, note2_recv):
    widths, snaps, cols, entries = sizes
    q = lax.axis_index("snap")
    zlo, x, y, core = (lax.axis_index(a) for a in PARAM)
    line = (q * 2 + zlo) * 2 + core
    plane = x * 4 + y

    def line_peer(k):
        p = (line + k) % 16
        return p, {"snap": p // 4, "zlo": (p // 2) % 2, "core": p % 2}

    def plane_peer(k):
        p = (plane + k) % 16
        return p, {"x": p // 4, "y": p % 4}

    barrier = pltpu.get_barrier_semaphore()

    def load(k):
        kind, i = k // 4, k % 4
        tile, way = tile_of(i)
        block = (q + jnp.where(kind == 0, 2, jnp.where(kind == 1, 4 - way, jnp.where(kind == 2, 4 + way, 0)))) % 4
        return pltpu.make_async_copy(
            snap_hbm.at[:, pl.ds(pl.multiple_of(tile * ROWS, ROWS), ROWS),
                        pl.ds(pl.multiple_of(block * cols, cols), cols)],
            stage.at[k], stage_sem.at[k])

    load(0).start()
    coef_copy = pltpu.make_async_copy(coeffs_hbm, coef, coef_sem)
    coef_copy.start()
    for k in range(1, 16):
        _, peer = line_peer(k)
        pl.semaphore_signal(barrier, inc=1, device_id=peer, device_id_type=MESH)
        _, peer = plane_peer(k)
        pl.semaphore_signal(barrier, inc=1, device_id=peer, device_id_type=MESH)
    for k in range(1, 16):
        load(k).start()

    coef_copy.wait()
    part = coef[...]
    m, n = widths * ROWS, snaps * ROWS
    up = jnp.where(lax.broadcasted_iota(jnp.int32, (m, widths), 0) // ROWS
                   == lax.broadcasted_iota(jnp.int32, (m, widths), 1), 1.0, 0.0).astype(jnp.bfloat16)
    across = jnp.where(lax.broadcasted_iota(jnp.int32, (snaps, n), 1) // ROWS
                       == lax.broadcasted_iota(jnp.int32, (snaps, n), 0), 1.0, 0.0).astype(jnp.bfloat16)
    same = (lax.broadcasted_iota(jnp.int32, (m, n), 0) % ROWS
            == lax.broadcasted_iota(jnp.int32, (m, n), 1) % ROWS)
    for half in range(2):
        top = part.astype(jnp.bfloat16)
        part = part - top.astype(jnp.float32)
        spread = jnp.dot(up, top, preferred_element_type=jnp.float32).astype(jnp.bfloat16)
        spread = jnp.dot(spread, across, preferred_element_type=jnp.float32)
        kron[pl.ds(half * m, m), :] = jnp.where(same, spread, 0.0).astype(jnp.bfloat16)

    def product(k):
        load(k).wait()
        both = jnp.dot(kron[...], stage[k].reshape(n, cols), preferred_element_type=jnp.float32)
        return (both[:m] + both[m:]).reshape(widths, ROWS, cols)

    def copies(k, target):
        peer = {"snap": (q + target + 4) % 4}
        return (
            pltpu.make_async_remote_copy(
                src_ref=sent_max.at[k], dst_ref=got_max.at[k], send_sem=send_max_sem.at[k],
                recv_sem=recv_max_sem.at[k], device_id=peer, device_id_type=MESH),
            pltpu.make_async_remote_copy(
                src_ref=sent.at[k], dst_ref=got.at[k], send_sem=send_sem.at[k],
                recv_sem=recv_sem.at[k], device_id=peer, device_id_type=MESH),
        )

    def put(k, value):
        sent[k], sent_max[k] = encode(value)

    def send(k, target):
        for copy in copies(k, target):
            copy.start()

    def receive(k):
        for copy in copies(k, 1):
            copy.wait_recv()
        return decode(got[k], got_max[k])

    put(0, product(0))
    pl.semaphore_wait(barrier, 30)
    send(0, -1)

    def first(k, _):
        tile, way = tile_of(k % 4)
        put(k, product(k))
        send(k, jnp.where(k < 4, way, -way))
        return 0

    lax.fori_loop(1, 8, first, 0)

    def mine(i, _):
        total[i] = product(12 + i)
        return 0

    lax.fori_loop(0, 4, mine, 0)

    def forward(i, _):
        tile, way = tile_of(i)
        put(8 + i, product(8 + i) + receive(i))
        send(8 + i, way)
        return 0

    lax.fori_loop(0, 4, forward, 0)

    def direct(i, _):
        total[i] = total[i] + receive(4 + i)
        return 0

    lax.fori_loop(0, 4, direct, 0)
    squares[...] = jnp.zeros_like(squares)

    def out(i):
        tile, way = tile_of(i)
        return pltpu.make_async_copy(
            total.at[i], avg_hbm.at[:, pl.ds(pl.multiple_of(tile * ROWS, ROWS), ROWS), :], out_sem.at[i])

    def last(i, _):
        value = total[i] + receive(8 + i)
        total[i] = value
        out(i).start()
        squares[...] += jnp.sum(value * value, axis=1)
        return 0

    lax.fori_loop(0, 4, last, 0)

    per = jnp.sum(squares[...], axis=1, keepdims=True)
    spot = (lax.broadcasted_iota(jnp.int32, (widths, 128), 0)
            == lax.broadcasted_iota(jnp.int32, (widths, 128), 1))
    value = jnp.sum(jnp.where(spot, per, 0.0), axis=0, keepdims=True)
    for step, (here, peer_of, seen, ssem, rsem) in enumerate((
            (line, line_peer, seen1, note1_send, note1_recv),
            (plane, plane_peer, seen2, note2_send, note2_recv))):
        note[step] = value
        seen[here] = value

        def message(k):
            p, peer = peer_of(k)
            return p, pltpu.make_async_remote_copy(
                src_ref=note.at[step], dst_ref=seen.at[here], send_sem=ssem.at[k - 1],
                recv_sem=rsem.at[here], device_id=peer, device_id_type=MESH)

        for k in range(1, 16):
            message(k)[1].start()
        for k in range(1, 16):
            p, _ = peer_of(k)
            pltpu.make_async_remote_copy(
                src_ref=note.at[step], dst_ref=seen.at[p], send_sem=ssem.at[k - 1],
                recv_sem=rsem.at[p], device_id=peer_of(k)[1], device_id_type=MESH).wait_recv()
        value = jnp.sum(seen[...], axis=0)
    norm_ref[...] = jnp.sqrt(value / jnp.float32(entries))

    for step, (peer_of, seen, ssem, rsem, here) in enumerate((
            (line_peer, seen1, note1_send, note1_recv, line),
            (plane_peer, seen2, note2_send, note2_recv, plane))):
        for k in range(1, 16):
            pltpu.make_async_remote_copy(
                src_ref=note.at[step], dst_ref=seen.at[here], send_sem=ssem.at[k - 1],
                recv_sem=rsem.at[here], device_id=peer_of(k)[1], device_id_type=MESH).wait_send()

    def drain(k, _):
        for copy in copies(k, 1):
            copy.wait_send()
        return 0

    lax.fori_loop(0, 12, drain, 0)
    for i in range(4):
        out(i).wait()


def on_device(snapshots, coeffs):
    widths, snaps = coeffs.shape
    _, rows, all_cols = snapshots.shape
    cols = all_cols // 4
    entries = rows * all_cols * 64
    pieces = 16
    averages, norms = pl.pallas_call(
        functools.partial(kernel, (widths, snaps, cols, entries)),
        out_shape=(jax.ShapeDtypeStruct((widths, rows, cols), jnp.float32),
                   jax.ShapeDtypeStruct((1, 128), jnp.float32)),
        in_specs=[pl.BlockSpec(memory_space=pl.ANY)] * 2,
        out_specs=(pl.BlockSpec(memory_space=pl.ANY), pl.BlockSpec(memory_space=pltpu.VMEM)),
        scratch_shapes=[
            pltpu.VMEM((widths, snaps), jnp.float32),
            pltpu.VMEM((pieces, snaps, ROWS, cols), jnp.bfloat16),
            pltpu.VMEM((2 * widths * ROWS, snaps * ROWS), jnp.bfloat16),
            pltpu.VMEM((4, widths, ROWS, cols), jnp.float32),
            pltpu.VMEM((12, widths, ROWS, cols), jnp.bfloat16),
            pltpu.VMEM((12, 1, cols), jnp.float32),
            pltpu.VMEM((12, widths, ROWS, cols), jnp.bfloat16),
            pltpu.VMEM((12, 1, cols), jnp.float32),
            pltpu.VMEM((4, widths, ROWS, cols), jnp.float32),
            pltpu.VMEM((widths, cols), jnp.float32),
            pltpu.VMEM((2, 1, 128), jnp.float32),
            pltpu.VMEM((16, 1, 128), jnp.float32),
            pltpu.VMEM((16, 1, 128), jnp.float32),
            pltpu.SemaphoreType.DMA,
            pltpu.SemaphoreType.DMA((pieces,)),
            pltpu.SemaphoreType.DMA((4,)),
            pltpu.SemaphoreType.DMA((12,)),
            pltpu.SemaphoreType.DMA((12,)),
            pltpu.SemaphoreType.DMA((12,)),
            pltpu.SemaphoreType.DMA((12,)),
            pltpu.SemaphoreType.DMA((15,)),
            pltpu.SemaphoreType.DMA((16,)),
            pltpu.SemaphoreType.DMA((15,)),
            pltpu.SemaphoreType.DMA((16,)),
        ],
        compiler_params=pltpu.CompilerParams(collective_id=0, has_side_effects=True),
    )(coeffs, snapshots)
    return averages, norms[0, :widths]


def solution(mesh):
    split = Mesh(mesh.devices.reshape(mesh.shape["snap"], 2, 4, 4, 2), ("snap",) + PARAM)
    return jax.shard_map(
        on_device,
        mesh=split,
        in_specs=(P("snap", PARAM, None), P(None, "snap")),
        out_specs=(P(None, PARAM, "snap"), P()),
        check_vma=False,
    )
```

time: 165 us -> 62.9 us (0.38)
  waiting for transfers between devices: 88.4 us -> 0 us
  Pallas kernels: 0 us -> 58.7 us
  blocking collectives: 39.6 us -> 0 us
  matrix products: 17.1 us -> 0 us
  between operations: 14 us -> 0.64 us
  other arithmetic: 1.99 us -> 0 us
    reduce_scatter x1 -> x0, waiting for transfers between devices: 88.4 us -> none  [on_device(): lax.psum_scatter(partial_value, 'snap', scatter_dimension=2, tiled=True)]
    pallas_call x0 -> x1, Pallas kernels: none -> 58.7 us  [on_device(): pl.pallas_call(functools.partial(kernel, (widths, snaps, cols, entries)),...]
    psum x5 -> x0, blocking collectives: 39.6 us -> none  [one_axis_at_a_time(): return functools.reduce(lax.psum, axes, shard)]
    dot_general x1 -> x0, matrix products: 17.1 us -> none  [combine(): jnp.dot(weights, flat, precision=lax.Precision.HIGHEST, preferred_element...]
    unnamed x3 -> x1, local copies, waits for them, and re-layouts: 3.45 us -> 2.29 us
  transfers between devices with their start and end apart: 1 -> 0, of which waited for: 1 -> 0; matrix products, arithmetic and copies ran while one was open for 0% -> 0% of each run, Pallas kernels for 0% -> 0%
where the time goes in v1:
time: 62.9 us; the launch traced here: 62.7 us
  Pallas kernels  58.7 us (93%)
  local copies, waits for them, and re-layouts  3.41 us (5%)
  between operations  0.64 us (1%)
    pallas_call x1, Pallas kernels, on_device(): pl.pallas_call(functools.partial(kernel, (widths, snaps, cols, entries)),...  58.7 us
    unnamed x1, local copies, waits for them, and re-layouts  2.29 us

profile of v1, /device:TPU:1, one launch (start us, length us, event | category | flops | bytes accessed | tf_op | source)
XLA Modules:
  0.0 62.7 jit_solution(4572472255556607350)
XLA Ops:
  0.6 58.7 %shard_map.41 = (f32[16,64,256]{2,1,0:T(8,128)}, f32[1,128]{1,0:T(1,128)}) custom-call(f32[16,64]{1,0:T(8,128)} %coeffs_hbm.1, bf16[64,64,1024]{2,1,0:T(8,128)(2,1)} %snap_hbm.1), custom_call_target="tpu_custom_call" | custom-call | tf_op jit(solution)/shard_map/pallas_call | solution.py:220
  59.3 1.1 %slice_bitcast_fusion = f32[16]{0:T(128)} fusion(f32[1,128]{1,0:T(1,128)} %get-tuple-element.5), kind=kLoop, calls=%fused_computation | loop fusion | bytes 128 | tf_op jit(solution)/shard_map/squeeze | solution.py:254
  60.4 2.3 %copy.5 = f32[16,64,256]{2,1,0:T(8,128)} copy(f32[16,64,256]{2,1,0:T(8,128)} %get-tuple-element.8) | data formatting | bytes 2097152

commit v2 on v1

--- a/solution.py
+++ b/solution.py
@@ -35,10 +35,10 @@
     return (i % 2) * 2 + i // 2, 2 * (i % 2) - 1
 
 
-def kernel(sizes, coeffs_hbm, snap_hbm, avg_hbm, norm_ref,
-           coef, stage, kron, share, sent, sent_max, got, got_max, total, squares,
+def kernel(sizes, coeffs_hbm, snap_hbm, avg_out, norm_out,
+           avg, norm, coef, stage, kron, sent, sent_max, got, got_max, squares,
            note, seen1, seen2,
-           coef_sem, stage_sem, out_sem, send_sem, send_max_sem, recv_sem, recv_max_sem,
+           coef_sem, stage_sem, out_sem, norm_sem, relay_sem, send_sem, send_max_sem, recv_sem, recv_max_sem,
            note1_send, note1_recv, note2_send, note2_recv):
     widths, snaps, cols, entries = sizes
     q = lax.axis_index("snap")
@@ -53,6 +53,13 @@
     def plane_peer(k):
         p = (plane + k) % 16
         return p, {"x": p // 4, "y": p % 4}
+
+    def line_at(dz, dc):
+        z = (q * 2 + zlo + dz + 8) % 8
+        return {"snap": z // 2, "zlo": z % 2, "core": (core + dc) % 2}
+
+    def plane_at(dx, dy):
+        return {"x": (x + dx + 4) % 4, "y": (y + dy + 4) % 4}
 
     barrier = pltpu.get_barrier_semaphore()
 
@@ -65,31 +72,30 @@
                         pl.ds(pl.multiple_of(block * cols, cols), cols)],
             stage.at[k], stage_sem.at[k])
 
-    load(0).start()
     coef_copy = pltpu.make_async_copy(coeffs_hbm, coef, coef_sem)
     coef_copy.start()
-    for k in range(1, 16):
-        _, peer = line_peer(k)
+    load(0).start()
+    load(1).start()
+    near = [line_at(dz, dc) for dz in (-2, 2, -1, 1, 0) for dc in (0, 1) if dz or dc]
+    near += [plane_at(dx, dy) for dx, dy in ((1, 0), (-1, 0), (2, 0), (0, 1), (0, -1), (0, 2),
+                                             (1, 1), (1, -1), (-1, 1), (-1, -1))]
+    for peer in near:
         pl.semaphore_signal(barrier, inc=1, device_id=peer, device_id_type=MESH)
-        _, peer = plane_peer(k)
-        pl.semaphore_signal(barrier, inc=1, device_id=peer, device_id_type=MESH)
-    for k in range(1, 16):
+    for k in range(2, 16):
         load(k).start()
 
-    coef_copy.wait()
-    part = coef[...]
     m, n = widths * ROWS, snaps * ROWS
-    up = jnp.where(lax.broadcasted_iota(jnp.int32, (m, widths), 0) // ROWS
-                   == lax.broadcasted_iota(jnp.int32, (m, widths), 1), 1.0, 0.0).astype(jnp.bfloat16)
     across = jnp.where(lax.broadcasted_iota(jnp.int32, (snaps, n), 1) // ROWS
                        == lax.broadcasted_iota(jnp.int32, (snaps, n), 0), 1.0, 0.0).astype(jnp.bfloat16)
     same = (lax.broadcasted_iota(jnp.int32, (m, n), 0) % ROWS
             == lax.broadcasted_iota(jnp.int32, (m, n), 1) % ROWS)
+    with jax.named_scope("coef_wait"):
+        coef_copy.wait()
+    part = jnp.broadcast_to(coef[...][:, None, :], (widths, ROWS, snaps)).reshape(m, snaps)
     for half in range(2):
         top = part.astype(jnp.bfloat16)
         part = part - top.astype(jnp.float32)
-        spread = jnp.dot(up, top, preferred_element_type=jnp.float32).astype(jnp.bfloat16)
-        spread = jnp.dot(spread, across, preferred_element_type=jnp.float32)
+        spread = jnp.dot(top, across, preferred_element_type=jnp.float32)
         kron[pl.ds(half * m, m), :] = jnp.where(same, spread, 0.0).astype(jnp.bfloat16)
 
     def product(k):
@@ -120,9 +126,14 @@
             copy.wait_recv()
         return decode(got[k], got_max[k])
 
-    put(0, product(0))
-    pl.semaphore_wait(barrier, 30)
+    with jax.named_scope("product0"):
+        put(0, product(0))
+    with jax.named_scope("barrier"):
+        pl.semaphore_wait(barrier, len(near))
     send(0, -1)
+    relays = [line_at(-2, 0), line_at(2, 0), plane_at(2, 0), plane_at(0, 2)]
+    for peer in relays:
+        pl.semaphore_signal(relay_sem, inc=1, device_id=peer, device_id_type=MESH)
 
     def first(k, _):
         tile, way = tile_of(k % 4)
@@ -130,13 +141,18 @@
         send(k, jnp.where(k < 4, way, -way))
         return 0
 
-    lax.fori_loop(1, 8, first, 0)
+    with jax.named_scope("first"):
+        lax.fori_loop(1, 8, first, 0)
+
+    def rows_of(i):
+        return pl.ds(pl.multiple_of(tile_of(i)[0] * ROWS, ROWS), ROWS)
 
     def mine(i, _):
-        total[i] = product(12 + i)
-        return 0
-
-    lax.fori_loop(0, 4, mine, 0)
+        avg[:, rows_of(i), :] = product(12 + i)
+        return 0
+
+    with jax.named_scope("mine"):
+        lax.fori_loop(0, 4, mine, 0)
 
     def forward(i, _):
         tile, way = tile_of(i)
@@ -144,28 +160,30 @@
         send(8 + i, way)
         return 0
 
-    lax.fori_loop(0, 4, forward, 0)
+    with jax.named_scope("forward"):
+        lax.fori_loop(0, 4, forward, 0)
 
     def direct(i, _):
-        total[i] = total[i] + receive(4 + i)
-        return 0
-
-    lax.fori_loop(0, 4, direct, 0)
+        avg[:, rows_of(i), :] += receive(4 + i)
+        return 0
+
+    with jax.named_scope("direct"):
+        lax.fori_loop(0, 4, direct, 0)
     squares[...] = jnp.zeros_like(squares)
-
-    def out(i):
-        tile, way = tile_of(i)
-        return pltpu.make_async_copy(
-            total.at[i], avg_hbm.at[:, pl.ds(pl.multiple_of(tile * ROWS, ROWS), ROWS), :], out_sem.at[i])
+    with jax.named_scope("relay"):
+        pl.semaphore_wait(relay_sem, len(relays))
 
     def last(i, _):
-        value = total[i] + receive(8 + i)
-        total[i] = value
-        out(i).start()
+        value = avg[:, rows_of(i), :] + receive(8 + i)
+        avg[:, rows_of(i), :] = value
         squares[...] += jnp.sum(value * value, axis=1)
         return 0
 
-    lax.fori_loop(0, 4, last, 0)
+    with jax.named_scope("last"):
+        lax.fori_loop(0, 4, last, 0)
+
+    out = pltpu.make_async_copy(avg, avg_out, out_sem)
+    out.start()
 
     per = jnp.sum(squares[...], axis=1, keepdims=True)
     spot = (lax.broadcasted_iota(jnp.int32, (widths, 128), 0)
@@ -191,7 +209,9 @@
                 src_ref=note.at[step], dst_ref=seen.at[p], send_sem=ssem.at[k - 1],
                 recv_sem=rsem.at[p], device_id=peer_of(k)[1], device_id_type=MESH).wait_recv()
         value = jnp.sum(seen[...], axis=0)
-    norm_ref[...] = jnp.sqrt(value / jnp.float32(entries))
+    norm[...] = jnp.sqrt(value / jnp.float32(entries))
+    norm_copy = pltpu.make_async_copy(norm, norm_out, norm_sem)
+    norm_copy.start()
 
     for step, (peer_of, seen, ssem, rsem, here) in enumerate((
             (line_peer, seen1, note1_send, note1_recv, line),
@@ -206,9 +226,17 @@
             copy.wait_send()
         return 0
 
-    lax.fori_loop(0, 12, drain, 0)
-    for i in range(4):
-        out(i).wait()
+    with jax.named_scope("drain"):
+        lax.fori_loop(0, 12, drain, 0)
+    out.wait()
+    norm_copy.wait()
+
+
+def write(avg, norm, avg_hbm, norm_out, sem):
+    copy = pltpu.make_async_copy(avg, avg_hbm, sem)
+    copy.start()
+    norm_out[...] = norm[0, :norm_out.shape[0]]
+    copy.wait()
 
 
 def on_device(snapshots, coeffs):
@@ -219,27 +247,28 @@
     pieces = 16
     averages, norms = pl.pallas_call(
         functools.partial(kernel, (widths, snaps, cols, entries)),
-        out_shape=(jax.ShapeDtypeStruct((widths, rows, cols), jnp.float32),
-                   jax.ShapeDtypeStruct((1, 128), jnp.float32)),
+        out_shape=(pltpu.VMEM((widths, rows, cols), jnp.float32), pltpu.VMEM((1, 128), jnp.float32)),
         in_specs=[pl.BlockSpec(memory_space=pl.ANY)] * 2,
-        out_specs=(pl.BlockSpec(memory_space=pl.ANY), pl.BlockSpec(memory_space=pltpu.VMEM)),
+        out_specs=[pl.BlockSpec(memory_space=pl.ANY)] * 2,
         scratch_shapes=[
+            pltpu.VMEM((widths, rows, cols), jnp.float32),
+            pltpu.VMEM((1, 128), jnp.float32),
             pltpu.VMEM((widths, snaps), jnp.float32),
             pltpu.VMEM((pieces, snaps, ROWS, cols), jnp.bfloat16),
             pltpu.VMEM((2 * widths * ROWS, snaps * ROWS), jnp.bfloat16),
-            pltpu.VMEM((4, widths, ROWS, cols), jnp.float32),
             pltpu.VMEM((12, widths, ROWS, cols), jnp.bfloat16),
             pltpu.VMEM((12, 1, cols), jnp.float32),
             pltpu.VMEM((12, widths, ROWS, cols), jnp.bfloat16),
             pltpu.VMEM((12, 1, cols), jnp.float32),
-            pltpu.VMEM((4, widths, ROWS, cols), jnp.float32),
             pltpu.VMEM((widths, cols), jnp.float32),
             pltpu.VMEM((2, 1, 128), jnp.float32),
             pltpu.VMEM((16, 1, 128), jnp.float32),
             pltpu.VMEM((16, 1, 128), jnp.float32),
             pltpu.SemaphoreType.DMA,
             pltpu.SemaphoreType.DMA((pieces,)),
-            pltpu.SemaphoreType.DMA((4,)),
+            pltpu.SemaphoreType.DMA,
+            pltpu.SemaphoreType.DMA,
+            pltpu.SemaphoreType.REGULAR,
             pltpu.SemaphoreType.DMA((12,)),
             pltpu.SemaphoreType.DMA((12,)),
             pltpu.SemaphoreType.DMA((12,)),
@@ -251,7 +280,15 @@
         ],
         compiler_params=pltpu.CompilerParams(collective_id=0, has_side_effects=True),
     )(coeffs, snapshots)
-    return averages, norms[0, :widths]
+    return pl.pallas_call(
+        write,
+        out_shape=(jax.ShapeDtypeStruct((widths, rows, cols), jnp.float32),
+                   jax.ShapeDtypeStruct((widths,), jnp.float32)),
+        in_specs=[pl.BlockSpec(memory_space=pl.ANY), pl.BlockSpec(memory_space=pltpu.VMEM)],
+        out_specs=(pl.BlockSpec(memory_space=pl.ANY), pl.BlockSpec(memory_space=pltpu.VMEM)),
+        scratch_shapes=[pltpu.SemaphoreType.DMA],
+    )(pltpu.with_memory_space_constraint(averages, pltpu.VMEM),
+      pltpu.with_memory_space_constraint(norms, pltpu.VMEM))
 
 
 def solution(mesh):

time: 62.9 us -> 59.3 us (0.943)
  local copies, waits for them, and re-layouts: 3.41 us -> 0 us
    unnamed x1 -> x0, local copies, waits for them, and re-layouts: 2.29 us -> none
    pallas_call x1, Pallas kernels: 58.7 us -> 57 us  [on_device(): pl.pallas_call(functools.partial(kernel, (widths, snaps, cols, entries)),...]
    pallas_call x0 -> x1, Pallas kernels: none -> 1.49 us  [on_device(): pl.pallas_call(write, out_shape=(jax.ShapeDtypeStruct((widths, rows, cols...]
    squeeze x1 -> x0, local copies, waits for them, and re-layouts: 1.11 us -> none  [on_device(): return (averages, norms[0, :widths])]
where the time goes in v2:
time: 59.3 us; the launch traced here: 59.1 us
  Pallas kernels  58.5 us (99%)
  between operations  0.64 us (1%)
    pallas_call x1, Pallas kernels, on_device(): pl.pallas_call(functools.partial(kernel, (widths, snaps, cols, entries)),...  57 us
    pallas_call x1, Pallas kernels, on_device(): pl.pallas_call(write, out_shape=(jax.ShapeDtypeStruct((widths, rows, cols...  1.49 us

profile of v2, /device:TPU:1, one launch (start us, length us, event | category | flops | bytes accessed | tf_op | source)
XLA Modules:
  0.0 59.1 jit_solution(9404228786096487332)
XLA Ops:
  0.6 57.0 %shard_map.41 = (f32[16,64,256]{2,1,0:T(8,128)S(1)}, f32[1,128]{1,0:T(1,128)S(1)}) custom-call(f32[16,64]{1,0:T(8,128)} %coeffs_hbm.1, bf16[64,64,1024]{2,1,0:T(8,128)(2,1)} %snap_hbm.1), custom_call_target="tpu_custom_call" | custom-call | tf_op jit(solution)/shard_map/pallas_call | solution.py:248
  57.7 1.5 %shard_map.42 = (f32[16,64,256]{2,1,0:T(8,128)}, f32[16]{0:T(128)}) custom-call(f32[16,64,256]{2,1,0:T(8,128)S(1)} %get-tuple-element.4.avg, f32[1,128]{1,0:T(1,128)S(1)} %get-tuple-element.5.norm), custom_call_target="tpu_custom_call" | custom-call | tf_op jit(solution)/shard_map/pallas_call | solution.py:283

commit v3 on v2

v3 whole, which is shorter than its diff:
```python
import functools

import jax
import jax.numpy as jnp
from jax import lax
from jax.experimental import pallas as pl
from jax.experimental.pallas import tpu as pltpu
from jax.sharding import Mesh
from jax.sharding import PartitionSpec as P

MESH = pl.DeviceIdType.MESH
PARAM = ("zlo", "x", "y", "core")
ROWS = 16
HALF = 8
LEAST = -125.0
SPAN = 251.5
TINY = 1e-37
PIECES = 12
Z_FAR = (4, 3, -3, 2, -2, 1, -1, 0)
PLANE_FAR = tuple(sorted(((dx, dy) for dx in (-1, 0, 1, 2) for dy in (-1, 0, 1, 2)),
                         key=lambda d: -abs(d[0]) - abs(d[1])))


def encode(value):
    size = jnp.abs(value)
    largest = jnp.max(jnp.max(jnp.max(size, axis=0), axis=0), axis=0, keepdims=True)[None]
    largest = jnp.maximum(largest, TINY)
    inverse = 1.0 / largest
    power = jnp.exp2((size * inverse[:, None]) * SPAN + LEAST)
    return jnp.where(value < 0, -power, power).astype(jnp.bfloat16), largest


def decode(codes, largest):
    code = codes.astype(jnp.float32)
    size = (jnp.log2(jnp.abs(code)) - LEAST) * (largest * (1.0 / SPAN))[:, None]
    return jnp.where(code < 0, -size, size)


def tile_of(i):
    return (i % 2) * 2 + i // 2, 2 * (i % 2) - 1


def kernel(sizes, coeffs_hbm, snap_hbm, avg_out, norm_out,
           avg, norm, coef, stage, kron, sent, sent_max, got, got_max, piece, squares,
           note, seen1, seen2,
           coef_sem, stage_sem, out_sem, norm_sem, relay_sem, send_sem, send_max_sem,
           recv_sem, note_send, note_recv):
    widths, snaps, cols, entries = sizes
    halves = widths // HALF
    q = lax.axis_index("snap")
    zlo, x, y, core = (lax.axis_index(a) for a in PARAM)
    line = (q * 2 + zlo) * 2 + core
    plane = x * 4 + y

    def line_at(dz, to_core):
        z = (q * 2 + zlo + dz + 8) % 8
        return {"snap": z // 2, "zlo": z % 2, "core": to_core}

    def plane_at(dx, dy, to_core):
        return {"x": (x + dx + 4) % 4, "y": (y + dy + 4) % 4, "core": to_core}

    barrier = pltpu.get_barrier_semaphore()

    def load(k, group):
        kind, i = k // 4, k % 4
        tile, way = tile_of(i)
        block = (q + jnp.where(kind == 0, 2, jnp.where(kind == 1, 4 - way, jnp.where(kind == 2, 4 + way, 0)))) % 4
        return pltpu.make_async_copy(
            snap_hbm.at[:, pl.ds(pl.multiple_of(tile * ROWS, ROWS), ROWS),
                        pl.ds(pl.multiple_of(block * cols, cols), cols)],
            stage.at[k], stage_sem.at[group])

    coef_copy = pltpu.make_async_copy(coeffs_hbm, coef, coef_sem)
    coef_copy.start()
    load(0, 0).start()
    load(1, 1).start()
    near = [line_at(dz, core if same else 1 - core)
            for dz in (-2, 2, -1, 1, 0) for same in (True, False) if dz or not same]
    near += [plane_at(dx, dy, core if same else 1 - core)
             for dx, dy in PLANE_FAR if 0 < abs(dx) + abs(dy) <= 2 for same in (True, False)]
    for peer in near:
        pl.semaphore_signal(barrier, inc=1, device_id=peer, device_id_type=MESH)
    for k in range(2, 16):
        load(k, 2 + (k > 3) + (k > 7) + (k > 11)).start()

    m, n = HALF * ROWS, snaps * ROWS
    across = jnp.where(lax.broadcasted_iota(jnp.int32, (snaps, n), 1) // ROWS
                       == lax.broadcasted_iota(jnp.int32, (snaps, n), 0), 1.0, 0.0).astype(jnp.bfloat16)
    same = jnp.where(lax.broadcasted_iota(jnp.int32, (m, n), 0) % ROWS
                     == lax.broadcasted_iota(jnp.int32, (m, n), 1) % ROWS, 1.0, 0.0).astype(jnp.bfloat16)
    with jax.named_scope("coef_wait"):
        coef_copy.wait()
    part = jnp.broadcast_to(coef[...][:, None, :], (widths, ROWS, snaps)).reshape(widths * ROWS, snaps)
    for p in range(2):
        top = part.astype(jnp.bfloat16)
        part = part - top.astype(jnp.float32)
        spread = jnp.dot(top, across, preferred_element_type=jnp.float32).astype(jnp.bfloat16)
        for h in range(halves):
            kron[pl.ds((h * 2 + p) * m, m), :] = spread[h * m:(h + 1) * m] * same

    def product(k):
        both = jnp.dot(kron[...], stage[k].reshape(n, cols), preferred_element_type=jnp.float32)
        both = both.reshape(halves, 2, HALF, ROWS, cols)
        return both[:, 0] + both[:, 1]

    def copies(k, target):
        peer = {"snap": (q + target + 4) % 4}
        return (
            pltpu.make_async_remote_copy(
                src_ref=sent_max.at[k], dst_ref=got_max.at[k], send_sem=send_max_sem,
                recv_sem=recv_sem.at[k], device_id=peer, device_id_type=MESH),
            pltpu.make_async_remote_copy(
                src_ref=sent.at[k], dst_ref=got.at[k], send_sem=send_sem,
                recv_sem=recv_sem.at[k], device_id=peer, device_id_type=MESH),
        )

    def put(k, value):
        sent[k], sent_max[k] = encode(value)

    def send(k, target):
        for copy in copies(k, target):
            copy.start()

    def receive(k):
        pltpu.make_async_copy(piece, piece, recv_sem.at[k]).wait()
        return decode(got[k], got_max[k]).reshape(widths, ROWS, cols)

    load(0, 0).wait()
    put(0, product(0))
    with jax.named_scope("barrier"):
        pl.semaphore_wait(barrier, len(near))
    send(0, -1)

    def first(k, _):
        tile, way = tile_of(k % 4)
        put(k, product(k))
        send(k, jnp.where(k < 4, way, -way))
        return 0

    def loaded(k, count, group):
        pltpu.make_async_copy(stage.at[pl.ds(k, count)], stage.at[pl.ds(k, count)], stage_sem.at[group]).wait()

    with jax.named_scope("first"):
        load(1, 1).wait()
        lax.fori_loop(1, 2, first, 0)
        loaded(2, 2, 2)
        lax.fori_loop(2, 4, first, 0)
        loaded(4, 4, 3)
        lax.fori_loop(4, 8, first, 0)

    relays = [line_at(-2, core), line_at(2, core), plane_at(2, 0, core), plane_at(0, 2, core)]
    for peer in relays:
        pl.semaphore_signal(relay_sem, inc=1, device_id=peer, device_id_type=MESH)

    def rows_of(i):
        return pl.ds(pl.multiple_of(tile_of(i)[0] * ROWS, ROWS), ROWS)

    def mine(i, _):
        avg[:, rows_of(i), :] = product(12 + i).reshape(widths, ROWS, cols)
        return 0

    loaded(8, 4, 4)
    loaded(12, 4, 5)
    with jax.named_scope("mine"):
        lax.fori_loop(0, 4, mine, 0)

    def forward(i, _):
        tile, way = tile_of(i)
        put(8 + i, product(8 + i) + receive(i).reshape(halves, HALF, ROWS, cols))
        send(8 + i, way)
        return 0

    with jax.named_scope("forward"):
        lax.fori_loop(0, 4, forward, 0)

    def direct(i, _):
        avg[:, rows_of(i), :] += receive(4 + i)
        return 0

    with jax.named_scope("direct"):
        lax.fori_loop(0, 4, direct, 0)
    squares[...] = jnp.zeros_like(squares)
    with jax.named_scope("relay"):
        pl.semaphore_wait(relay_sem, len(relays))

    def last(i, _):
        value = avg[:, rows_of(i), :] + receive(8 + i)
        avg[:, rows_of(i), :] = value
        squares[...] += jnp.sum(value * value, axis=1)
        return 0

    with jax.named_scope("last"):
        lax.fori_loop(0, 4, last, 0)
    out = pltpu.make_async_copy(avg, avg_out, out_sem)
    out.start()

    per = jnp.sum(squares[...], axis=1, keepdims=True)
    spot = (lax.broadcasted_iota(jnp.int32, (widths, 128), 0)
            == lax.broadcasted_iota(jnp.int32, (widths, 128), 1))
    value = jnp.sum(jnp.where(spot, per, 0.0), axis=0, keepdims=True)
    note[0] = value
    seen1[line] = value

    def message(step, seen, here, peer):
        return pltpu.make_async_remote_copy(
            src_ref=note.at[step], dst_ref=seen.at[here], send_sem=note_send.at[step],
            recv_sem=note_recv.at[step], device_id=peer, device_id_type=MESH)

    def landed(step, count):
        return pltpu.make_async_copy(seen2.at[pl.ds(0, count)], seen2.at[pl.ds(0, count)], note_recv.at[step])

    def left(step, count):
        return pltpu.make_async_copy(seen2.at[pl.ds(0, count)], seen2.at[pl.ds(0, count)], note_send.at[step])

    hub = core == 1
    for dz in Z_FAR[:-1]:
        message(0, seen1, line, line_at(dz, 1)).start()

    @pl.when(jnp.logical_not(hub))
    def _():
        message(0, seen1, line, line_at(0, 1)).start()

    with jax.named_scope("drain"):
        pltpu.make_async_copy(sent, sent, send_sem).wait()
        pltpu.make_async_copy(sent_max, sent_max, send_max_sem).wait()

    @pl.when(hub)
    def _():
        with jax.named_scope("norm0"):
            landed(0, 15).wait()
        total = jnp.sum(seen1[...], axis=0)
        note[1] = total
        seen2[plane] = total
        for dx, dy in PLANE_FAR[:-1]:
            for to in (0, 1):
                message(1, seen2, plane, plane_at(dx, dy, to)).start()
        message(1, seen2, plane, plane_at(0, 0, 0)).start()
        left(0, 7).wait()
        with jax.named_scope("norm1"):
            landed(1, 15).wait()

    @pl.when(jnp.logical_not(hub))
    def _():
        left(0, 8).wait()
        with jax.named_scope("norm1"):
            landed(1, 16).wait()

    norm[...] = jnp.sqrt(jnp.sum(seen2[...], axis=0) / jnp.float32(entries))[0, :widths]
    norm_copy = pltpu.make_async_copy(norm, norm_out, norm_sem)
    norm_copy.start()

    @pl.when(hub)
    def _():
        left(1, 16).wait()
        left(1, 15).wait()

    out.wait()
    norm_copy.wait()


def write(avg, norm, avg_hbm, norm_hbm, sems):
    large = pltpu.make_async_copy(avg, avg_hbm, sems.at[0])
    small = pltpu.make_async_copy(norm, norm_hbm, sems.at[1])
    large.start()
    small.start()
    small.wait()
    large.wait()


def on_device(snapshots, coeffs):
    widths, snaps = coeffs.shape
    _, rows, all_cols = snapshots.shape
    cols = all_cols // 4
    halves = widths // HALF
    entries = rows * all_cols * 64
    averages, norms = pl.pallas_call(
        functools.partial(kernel, (widths, snaps, cols, entries)),
        out_shape=(pltpu.VMEM((widths, rows, cols), jnp.float32), pltpu.VMEM((widths,), jnp.float32)),
        in_specs=[pl.BlockSpec(memory_space=pl.ANY)] * 2,
        out_specs=[pl.BlockSpec(memory_space=pl.ANY)] * 2,
        scratch_shapes=[
            pltpu.VMEM((widths, rows, cols), jnp.float32),
            pltpu.VMEM((widths,), jnp.float32),
            pltpu.VMEM((widths, snaps), jnp.float32),
            pltpu.VMEM((16, snaps, ROWS, cols), jnp.bfloat16),
            pltpu.VMEM((2 * widths * ROWS, snaps * ROWS), jnp.bfloat16),
            pltpu.VMEM((PIECES, halves, HALF, ROWS, cols), jnp.bfloat16),
            pltpu.VMEM((PIECES, 1, 1, cols), jnp.float32),
            pltpu.VMEM((PIECES, halves, HALF, ROWS, cols), jnp.bfloat16),
            pltpu.VMEM((PIECES, 1, 1, cols), jnp.float32),
            pltpu.VMEM((widths * ROWS // 2 + 1, 1, cols), jnp.float32),
            pltpu.VMEM((widths, cols), jnp.float32),
            pltpu.VMEM((2, 1, 128), jnp.float32),
            pltpu.VMEM((16, 1, 128), jnp.float32),
            pltpu.VMEM((16, 1, 128), jnp.float32),
            pltpu.SemaphoreType.DMA,
            pltpu.SemaphoreType.DMA((6,)),
            pltpu.SemaphoreType.DMA,
            pltpu.SemaphoreType.DMA,
            pltpu.SemaphoreType.REGULAR,
            pltpu.SemaphoreType.DMA,
            pltpu.SemaphoreType.DMA,
            pltpu.SemaphoreType.DMA((PIECES,)),
            pltpu.SemaphoreType.DMA((2,)),
            pltpu.SemaphoreType.DMA((2,)),
        ],
        compiler_params=pltpu.CompilerParams(collective_id=0, has_side_effects=True),
    )(coeffs, snapshots)
    return pl.pallas_call(
        write,
        out_shape=(jax.ShapeDtypeStruct((widths, rows, cols), jnp.float32),
                   jax.ShapeDtypeStruct((widths,), jnp.float32)),
        in_specs=[pl.BlockSpec(memory_space=pl.ANY)] * 2,
        out_specs=[pl.BlockSpec(memory_space=pl.ANY)] * 2,
        scratch_shapes=[pltpu.SemaphoreType.DMA((2,))],
    )(pltpu.with_memory_space_constraint(averages, pltpu.VMEM),
      pltpu.with_memory_space_constraint(norms, pltpu.VMEM))


def solution(mesh):
    split = Mesh(mesh.devices.reshape(mesh.shape["snap"], 2, 4, 4, 2), ("snap",) + PARAM)
    return jax.shard_map(
        on_device,
        mesh=split,
        in_specs=(P("snap", PARAM, None), P(None, "snap")),
        out_specs=(P(None, PARAM, "snap"), P()),
        check_vma=False,
    )
```

time: 59.3 us -> 57.8 us (0.975)
  Pallas kernels: 58.5 us -> 57.1 us
    pallas_call x1, Pallas kernels: 57 us -> 56.1 us  [on_device(): pl.pallas_call(functools.partial(kernel, (widths, snaps, cols, entries)),...]
where the time goes in v3:
time: 57.8 us; the launch traced here: 57.7 us
  Pallas kernels  57.1 us (99%)
  between operations  0.64 us (1%)
    pallas_call x1, Pallas kernels, on_device(): pl.pallas_call(functools.partial(kernel, (widths, snaps, cols, entries)),...  56.1 us

profile of v3, /device:TPU:1, one launch (start us, length us, event | category | flops | bytes accessed | tf_op | source)
XLA Modules:
  0.0 57.7 jit_solution(5190133365343406407)
XLA Ops:
  0.6 56.1 %shard_map.41 = (f32[16,64,256]{2,1,0:T(8,128)S(1)}, f32[16]{0:T(128)S(1)}) custom-call(f32[16,64]{1,0:T(8,128)} %coeffs_hbm.1, bf16[64,64,1024]{2,1,0:T(8,128)(2,1)} %snap_hbm.1), custom_call_target="tpu_custom_call" | custom-call | tf_op jit(solution)/shard_map/pallas_call | solution.py:276
  56.7 1.0 %shard_map.42 = (f32[16,64,256]{2,1,0:T(8,128)}, f32[16]{0:T(128)}) custom-call(f32[16,64,256]{2,1,0:T(8,128)S(1)} %get-tuple-element.4.avg, f32[16]{0:T(128)S(1)} %get-tuple-element.5.norm), custom_call_target="tpu_custom_call" | custom-call | tf_op jit(solution)/shard_map/pallas_call | solution.py:309

commit v4 on v3

--- a/solution.py
+++ b/solution.py
@@ -16,6 +16,7 @@
 SPAN = 251.5
 TINY = 1e-37
 PIECES = 12
+EARLY = ((0, 0, 0, 1),)
 Z_FAR = (4, 3, -3, 2, -2, 1, -1, 0)
 PLANE_FAR = tuple(sorted(((dx, dy) for dx in (-1, 0, 1, 2) for dy in (-1, 0, 1, 2)),
                          key=lambda d: -abs(d[0]) - abs(d[1])))
@@ -42,8 +43,8 @@
 
 def kernel(sizes, coeffs_hbm, snap_hbm, avg_out, norm_out,
            avg, norm, coef, stage, kron, sent, sent_max, got, got_max, piece, squares,
-           note, seen1, seen2,
-           coef_sem, stage_sem, out_sem, norm_sem, relay_sem, send_sem, send_max_sem,
+           note, seen1, seen2, seen,
+           coef_sem, stage_sem, out_sem, norm_sem, relay_sem, all_sem, send_sem, send_max_sem,
            recv_sem, note_send, note_recv):
     widths, snaps, cols, entries = sizes
     halves = widths // HALF
@@ -51,6 +52,7 @@
     zlo, x, y, core = (lax.axis_index(a) for a in PARAM)
     line = (q * 2 + zlo) * 2 + core
     plane = x * 4 + y
+    z = q * 2 + zlo
 
     def line_at(dz, to_core):
         z = (q * 2 + zlo + dz + 8) % 8
@@ -173,6 +175,10 @@
     with jax.named_scope("forward"):
         lax.fori_loop(0, 4, forward, 0)
 
+    pl.semaphore_wait(relay_sem, len(relays))
+    for dx, dy in PLANE_FAR[:-1]:
+        pl.semaphore_signal(all_sem, inc=1, device_id=plane_at(dx, dy, core), device_id_type=MESH)
+
     def direct(i, _):
         avg[:, rows_of(i), :] += receive(4 + i)
         return 0
@@ -181,7 +187,7 @@
         lax.fori_loop(0, 4, direct, 0)
     squares[...] = jnp.zeros_like(squares)
     with jax.named_scope("relay"):
-        pl.semaphore_wait(relay_sem, len(relays))
+        pl.semaphore_wait(all_sem, len(PLANE_FAR) - 1)
 
     def last(i, _):
         value = avg[:, rows_of(i), :] + receive(8 + i)
@@ -201,18 +207,28 @@
     note[0] = value
     seen1[line] = value
 
-    def message(step, seen, here, peer):
+    def message(step, there, here, peer):
         return pltpu.make_async_remote_copy(
-            src_ref=note.at[step], dst_ref=seen.at[here], send_sem=note_send.at[step],
+            src_ref=note.at[step % 2], dst_ref=there.at[here], send_sem=note_send.at[step],
             recv_sem=note_recv.at[step], device_id=peer, device_id_type=MESH)
 
-    def landed(step, count):
-        return pltpu.make_async_copy(seen2.at[pl.ds(0, count)], seen2.at[pl.ds(0, count)], note_recv.at[step])
-
-    def left(step, count):
-        return pltpu.make_async_copy(seen2.at[pl.ds(0, count)], seen2.at[pl.ds(0, count)], note_send.at[step])
+    def wait(sem, count):
+        pltpu.make_async_copy(seen.at[pl.ds(0, count)], seen.at[pl.ds(0, count)], sem).wait()
+
+    def line_sum(there, first):
+        total = there[first]
+        for i in range(1, 16):
+            total = total + there[first + i]
+        return total
 
     hub = core == 1
+    early = [(z == ez) & (x == ex) & (y == ey) & (core == ec) for ez, ex, ey, ec in EARLY]
+    is_early = functools.reduce(jnp.logical_or, early)
+    for me, (ez, ex, ey, ec) in zip(early, EARLY):
+        @pl.when(jnp.logical_not(me))
+        def _():
+            message(2, seen, plane * 16 + line,
+                    {"snap": ez // 2, "zlo": ez % 2, "x": ex, "y": ey, "core": ec}).start()
     for dz in Z_FAR[:-1]:
         message(0, seen1, line, line_at(dz, 1)).start()
 
@@ -224,26 +240,56 @@
         pltpu.make_async_copy(sent, sent, send_sem).wait()
         pltpu.make_async_copy(sent_max, sent_max, send_max_sem).wait()
 
+    def spread(skip):
+        for dx, dy in PLANE_FAR:
+            for to in (0, 1):
+                if (dx, dy) == (0, 0) and to == 1:
+                    continue
+                peer = plane_at(dx, dy, to)
+                known = [(z == ez) & (peer["x"] == ex) & (peer["y"] == ey) for ez, ex, ey, ec in EARLY if ec == to]
+                if skip and known:
+                    @pl.when(jnp.logical_not(functools.reduce(jnp.logical_or, known)))
+                    def _():
+                        message(1, seen2, plane, peer).start()
+                else:
+                    message(1, seen2, plane, peer).start()
+
+    planes = sorted({e[0] for e in EARLY})
+    early_plane = functools.reduce(jnp.logical_or, [z == ez for ez in planes])
+
     @pl.when(hub)
     def _():
         with jax.named_scope("norm0"):
-            landed(0, 15).wait()
-        total = jnp.sum(seen1[...], axis=0)
+            wait(note_recv.at[0], 15)
+        total = line_sum(seen1, 0)
         note[1] = total
         seen2[plane] = total
-        for dx, dy in PLANE_FAR[:-1]:
-            for to in (0, 1):
-                message(1, seen2, plane, plane_at(dx, dy, to)).start()
-        message(1, seen2, plane, plane_at(0, 0, 0)).start()
-        left(0, 7).wait()
+
+        @pl.when(early_plane)
+        def _():
+            spread(True)
+
+        @pl.when(jnp.logical_not(early_plane))
+        def _():
+            spread(False)
+
+    @pl.when(is_early)
+    def _():
+        seen[plane * 16 + line] = value
+        with jax.named_scope("norm2"):
+            wait(note_recv.at[2], 255)
+        for p in range(16):
+            seen2[p] = line_sum(seen, p * 16)
+
+    @pl.when(jnp.logical_not(is_early) & hub)
+    def _():
         with jax.named_scope("norm1"):
-            landed(1, 15).wait()
-
-    @pl.when(jnp.logical_not(hub))
-    def _():
-        left(0, 8).wait()
+            wait(note_recv.at[1], 15)
+
+    @pl.when(jnp.logical_not(is_early | hub))
+    def _():
         with jax.named_scope("norm1"):
-            landed(1, 16).wait()
+            wait(note_recv.at[1], 16)
 
     norm[...] = jnp.sqrt(jnp.sum(seen2[...], axis=0) / jnp.float32(entries))[0, :widths]
     norm_copy = pltpu.make_async_copy(norm, norm_out, norm_sem)
@@ -251,8 +297,40 @@
 
     @pl.when(hub)
     def _():
-        left(1, 16).wait()
-        left(1, 15).wait()
+        wait(note_send.at[0], 7)
+        for ez in planes:
+            @pl.when(z == ez)
+            def _():
+                others = [e for e in EARLY if e[0] == ez]
+                for me, e in zip(early, EARLY):
+                    if e in others and e[3] == 1:
+                        @pl.when(me)
+                        def _():
+                            wait(note_send.at[1], 31 - len(others) + 1)
+                hubs = [me for me, e in zip(early, EARLY) if e in others and e[3] == 1]
+                if hubs:
+                    @pl.when(jnp.logical_not(functools.reduce(jnp.logical_or, hubs)))
+                    def _():
+                        wait(note_send.at[1], 31 - len(others))
+                else:
+                    wait(note_send.at[1], 31 - len(others))
+
+        @pl.when(jnp.logical_not(early_plane))
+        def _():
+            wait(note_send.at[1], 31)
+
+    @pl.when(jnp.logical_not(hub))
+    def _():
+        wait(note_send.at[0], 8)
+
+    @pl.when(is_early)
+    def _():
+        if len(EARLY) > 1:
+            wait(note_send.at[2], len(EARLY) - 1)
+
+    @pl.when(jnp.logical_not(is_early))
+    def _():
+        wait(note_send.at[2], len(EARLY))
 
     out.wait()
     norm_copy.wait()
@@ -293,16 +371,18 @@
             pltpu.VMEM((2, 1, 128), jnp.float32),
             pltpu.VMEM((16, 1, 128), jnp.float32),
             pltpu.VMEM((16, 1, 128), jnp.float32),
+            pltpu.VMEM((256, 1, 128), jnp.float32),
             pltpu.SemaphoreType.DMA,
             pltpu.SemaphoreType.DMA((6,)),
             pltpu.SemaphoreType.DMA,
             pltpu.SemaphoreType.DMA,
             pltpu.SemaphoreType.REGULAR,
+            pltpu.SemaphoreType.REGULAR,
             pltpu.SemaphoreType.DMA,
             pltpu.SemaphoreType.DMA,
             pltpu.SemaphoreType.DMA((PIECES,)),
-            pltpu.SemaphoreType.DMA((2,)),
-            pltpu.SemaphoreType.DMA((2,)),
+            pltpu.SemaphoreType.DMA((3,)),
+            pltpu.SemaphoreType.DMA((3,)),
         ],
         compiler_params=pltpu.CompilerParams(collective_id=0, has_side_effects=True),
     )(coeffs, snapshots)

time: 57.8 us -> 56.7 us (0.981)
  Pallas kernels: 57.1 us -> 55.9 us
    pallas_call x1, Pallas kernels: 56.1 us -> 54.9 us  [on_device(): pl.pallas_call(functools.partial(kernel, (widths, snaps, cols, entries)),...]
where the time goes in v4:
time: 56.7 us; the launch traced here: 56.5 us
  Pallas kernels  55.9 us (99%)
  between operations  0.64 us (1%)
    pallas_call x1, Pallas kernels, on_device(): pl.pallas_call(functools.partial(kernel, (widths, snaps, cols, entries)),...  54.9 us

profile of v4, /device:TPU:1, one launch (start us, length us, event | category | flops | bytes accessed | tf_op | source)
XLA Modules:
  0.0 56.5 jit_solution(4410276966085111579)
XLA Ops:
  0.6 54.9 %shard_map.41 = (f32[16,64,256]{2,1,0:T(8,128)S(1)}, f32[16]{0:T(128)S(1)}) custom-call(f32[16,64]{1,0:T(8,128)} %coeffs_hbm.1, bf16[64,64,1024]{2,1,0:T(8,128)(2,1)} %snap_hbm.1), custom_call_target="tpu_custom_call" | custom-call | tf_op jit(solution)/shard_map/pallas_call | solution.py:354
  55.6 1.0 %shard_map.42 = (f32[16,64,256]{2,1,0:T(8,128)}, f32[16]{0:T(128)}) custom-call(f32[16,64,256]{2,1,0:T(8,128)S(1)} %get-tuple-element.4.avg, f32[16]{0:T(128)S(1)} %get-tuple-element.5.norm), custom_call_target="tpu_custom_call" | custom-call | tf_op jit(solution)/shard_map/pallas_call | solution.py:389

commit v5 on v4

--- a/solution.py
+++ b/solution.py
@@ -16,7 +16,7 @@
 SPAN = 251.5
 TINY = 1e-37
 PIECES = 12
-EARLY = ((0, 0, 0, 1),)
+EARLY = ((0, 0, 0, 1), (1, 0, 0, 1), (1, 0, 0, 0))
 Z_FAR = (4, 3, -3, 2, -2, 1, -1, 0)
 PLANE_FAR = tuple(sorted(((dx, dy) for dx in (-1, 0, 1, 2) for dy in (-1, 0, 1, 2)),
                          key=lambda d: -abs(d[0]) - abs(d[1])))
@@ -75,15 +75,14 @@
     coef_copy = pltpu.make_async_copy(coeffs_hbm, coef, coef_sem)
     coef_copy.start()
     load(0, 0).start()
-    load(1, 1).start()
     near = [line_at(dz, core if same else 1 - core)
             for dz in (-2, 2, -1, 1, 0) for same in (True, False) if dz or not same]
     near += [plane_at(dx, dy, core if same else 1 - core)
              for dx, dy in PLANE_FAR if 0 < abs(dx) + abs(dy) <= 2 for same in (True, False)]
     for peer in near:
         pl.semaphore_signal(barrier, inc=1, device_id=peer, device_id_type=MESH)
-    for k in range(2, 16):
-        load(k, 2 + (k > 3) + (k > 7) + (k > 11)).start()
+    for k in range(1, 16):
+        load(k, 1 + (k > 3) + (k > 7) + (k > 11)).start()
 
     m, n = HALF * ROWS, snaps * ROWS
     across = jnp.where(lax.broadcasted_iota(jnp.int32, (snaps, n), 1) // ROWS
@@ -143,11 +142,9 @@
         pltpu.make_async_copy(stage.at[pl.ds(k, count)], stage.at[pl.ds(k, count)], stage_sem.at[group]).wait()
 
     with jax.named_scope("first"):
-        load(1, 1).wait()
-        lax.fori_loop(1, 2, first, 0)
-        loaded(2, 2, 2)
-        lax.fori_loop(2, 4, first, 0)
-        loaded(4, 4, 3)
+        loaded(1, 3, 1)
+        lax.fori_loop(1, 4, first, 0)
+        loaded(4, 4, 2)
         lax.fori_loop(4, 8, first, 0)
 
     relays = [line_at(-2, core), line_at(2, core), plane_at(2, 0, core), plane_at(0, 2, core)]
@@ -161,8 +158,8 @@
         avg[:, rows_of(i), :] = product(12 + i).reshape(widths, ROWS, cols)
         return 0
 
-    loaded(8, 4, 4)
-    loaded(12, 4, 5)
+    loaded(8, 4, 3)
+    loaded(12, 4, 4)
     with jax.named_scope("mine"):
         lax.fori_loop(0, 4, mine, 0)
 
@@ -373,7 +370,7 @@
             pltpu.VMEM((16, 1, 128), jnp.float32),
             pltpu.VMEM((256, 1, 128), jnp.float32),
             pltpu.SemaphoreType.DMA,
-            pltpu.SemaphoreType.DMA((6,)),
+            pltpu.SemaphoreType.DMA((5,)),
             pltpu.SemaphoreType.DMA,
             pltpu.SemaphoreType.DMA,
             pltpu.SemaphoreType.REGULAR,

time: 56.7 us -> 56.4 us (level)
  no operation moved by 1% of the time
where the time goes in v5:
time: 56.4 us; the launch traced here: 56.3 us
  Pallas kernels  55.7 us (99%)
  between operations  0.64 us (1%)
    pallas_call x1, Pallas kernels, on_device(): pl.pallas_call(functools.partial(kernel, (widths, snaps, cols, entries)),...  54.7 us

profile of v5, /device:TPU:1, one launch (start us, length us, event | category | flops | bytes accessed | tf_op | source)
XLA Modules:
  0.0 56.3 jit_solution(7342678098122440198)
XLA Ops:
  0.6 54.7 %shard_map.41 = (f32[16,64,256]{2,1,0:T(8,128)S(1)}, f32[16]{0:T(128)S(1)}) custom-call(f32[16,64]{1,0:T(8,128)} %coeffs_hbm.1, bf16[64,64,1024]{2,1,0:T(8,128)(2,1)} %snap_hbm.1), custom_call_target="tpu_custom_call" | custom-call | tf_op jit(solution)/shard_map/pallas_call | solution.py:351
  55.3 1.0 %shard_map.42 = (f32[16,64,256]{2,1,0:T(8,128)}, f32[16]{0:T(128)}) custom-call(f32[16,64,256]{2,1,0:T(8,128)S(1)} %get-tuple-element.4.avg, f32[16]{0:T(128)S(1)} %get-tuple-element.5.norm), custom_call_target="tpu_custom_call" | custom-call | tf_op jit(solution)/shard_map/pallas_call | solution.py:386

commit v6 on v5

--- a/solution.py
+++ b/solution.py
@@ -189,7 +189,8 @@
     def last(i, _):
         value = avg[:, rows_of(i), :] + receive(8 + i)
         avg[:, rows_of(i), :] = value
-        squares[...] += jnp.sum(value * value, axis=1)
+        square = (value * value).reshape(widths, ROWS // 8, 8, cols)
+        squares[...] += jnp.sum(square, axis=1)
         return 0
 
     with jax.named_scope("last"):
@@ -197,7 +198,7 @@
     out = pltpu.make_async_copy(avg, avg_out, out_sem)
     out.start()
 
-    per = jnp.sum(squares[...], axis=1, keepdims=True)
+    per = jnp.sum(jnp.sum(squares[...], axis=1), axis=1, keepdims=True)
     spot = (lax.broadcasted_iota(jnp.int32, (widths, 128), 0)
             == lax.broadcasted_iota(jnp.int32, (widths, 128), 1))
     value = jnp.sum(jnp.where(spot, per, 0.0), axis=0, keepdims=True)
@@ -364,7 +365,7 @@
             pltpu.VMEM((PIECES, halves, HALF, ROWS, cols), jnp.bfloat16),
             pltpu.VMEM((PIECES, 1, 1, cols), jnp.float32),
             pltpu.VMEM((widths * ROWS // 2 + 1, 1, cols), jnp.float32),
-            pltpu.VMEM((widths, cols), jnp.float32),
+            pltpu.VMEM((widths, 8, cols), jnp.float32),
             pltpu.VMEM((2, 1, 128), jnp.float32),
             pltpu.VMEM((16, 1, 128), jnp.float32),
             pltpu.VMEM((16, 1, 128), jnp.float32),

time: 56.4 us -> 56.4 us (level)
  no operation moved by 1% of the time
where the time goes in v6:
time: 56.4 us; the launch traced here: 56.3 us
  Pallas kernels  55.7 us (99%)
  between operations  0.64 us (1%)
    pallas_call x1, Pallas kernels, on_device(): pl.pallas_call(functools.partial(kernel, (widths, snaps, cols, entries)),...  54.7 us

profile of v6, /device:TPU:1, one launch (start us, length us, event | category | flops | bytes accessed | tf_op | source)
XLA Modules:
  0.0 56.3 jit_solution(10505023509061987751)
XLA Ops:
  0.6 54.7 %shard_map.41 = (f32[16,64,256]{2,1,0:T(8,128)S(1)}, f32[16]{0:T(128)S(1)}) custom-call(f32[16,64]{1,0:T(8,128)} %coeffs_hbm.1, bf16[64,64,1024]{2,1,0:T(8,128)(2,1)} %snap_hbm.1), custom_call_target="tpu_custom_call" | custom-call | tf_op jit(solution)/shard_map/pallas_call | solution.py:352
  55.3 1.0 %shard_map.42 = (f32[16,64,256]{2,1,0:T(8,128)}, f32[16]{0:T(128)}) custom-call(f32[16,64,256]{2,1,0:T(8,128)S(1)} %get-tuple-element.4.avg, f32[16]{0:T(128)S(1)} %get-tuple-element.5.norm), custom_call_target="tpu_custom_call" | custom-call | tf_op jit(solution)/shard_map/pallas_call | solution.py:387
